TPU v7x, 32 devices: a whole 2x2x4 slice. The times are simulated.
32 devices in a mesh: rows: 4 (over z), tp: 4 (over y, x), unit: 2 (over core).
Axes of the slice: x: 2, y: 2, z: 4, core: 2. Of those that a mesh axis runs over, the one named last changes fastest.
Arguments:
- train_query: bfloat16 [4096, 2048], P(('unit', 'rows'), 'tp'), parts along dimension 0, may hold values from -0.125 to 0.125
- low_query: bfloat16 [4096, 64], P(('unit', 'rows')), parts along dimension 0, may hold values from -0.125 to 0.125
- high_query: bfloat16 [128, 2048], P('unit', 'tp'), parts along dimension 0, may hold values from -0.75 to 0.75
- train_key: bfloat16 [4096, 512], P(('unit', 'rows'), 'tp'), parts along dimension 0, may hold values from -0.125 to 0.125
- low_key: bfloat16 [4096, 64], P(('unit', 'rows')), parts along dimension 0, may hold values from -0.125 to 0.125
- high_key: bfloat16 [128, 512], P('unit', 'tp'), parts along dimension 0, may hold values from -0.75 to 0.75
- train_value: bfloat16 [4096, 512], P(('unit', 'rows'), 'tp'), parts along dimension 0, may hold values from -0.125 to 0.125
- low_value: bfloat16 [4096, 64], P(('unit', 'rows')), parts along dimension 0, may hold values from -0.125 to 0.125
- high_value: bfloat16 [128, 512], P('unit', 'tp'), parts along dimension 0, may hold values from -0.75 to 0.75
- norm_train: float32 [4096], P(('unit', 'rows', 'tp')), parts along dimension 0, may hold values from 0.25 to 1.75
- norm_step: float32 [4096], P(('unit', 'rows', 'tp')), parts along dimension 0, may hold values from -0.3 to 0.3
Outputs:
- final_query: bfloat16 [4096, 2048], P(('unit', 'tp')), parts along dimension 0
- final_key: bfloat16 [1024, 2048], P(('unit', 'tp')), parts along dimension 0
- final_value: bfloat16 [1024, 2048], P(('unit', 'tp')), parts along dimension 0
- serve_norm: bfloat16 [4096], P('unit'), parts along dimension 0
There are 2 independent parts, one for each index of `unit`. A program takes and returns all parts, laid end to end along the dimension named above; each array names one. Nothing has to cross between parts.
All inputs are finite; a program needn't handle non-finite values.
Results may differ from a plain program's by a relative error of at most 0.001.
Values may be sent and summed in bfloat16 or wider, within the bound.
A program may use at most 64 MiB of HBM per device.

v0:
```python
import jax
import jax.numpy as jnp
from jax import lax
from jax.sharding import PartitionSpec as P

mix_rate = 0.5


def shards(
    train_query,
    low_query,
    high_query,
    train_key,
    low_key,
    high_key,
    train_value,
    low_value,
    high_value,
    norm_train,
    norm_step,
):
    result_query = train_query.astype(jnp.float32) + mix_rate * jnp.dot(
        low_query, high_query, preferred_element_type=jnp.float32
    )
    result_key = train_key.astype(jnp.float32) + mix_rate * jnp.dot(
        low_key, high_key, preferred_element_type=jnp.float32
    )
    result_value = train_value.astype(jnp.float32) + mix_rate * jnp.dot(
        low_value, high_value, preferred_element_type=jnp.float32
    )
    narrow_query, narrow_key, narrow_value = (
        result_query.astype(jnp.bfloat16),
        result_key.astype(jnp.bfloat16),
        result_value.astype(jnp.bfloat16),
    )
    final_query, final_key, final_value = (
        lax.all_gather(narrow_query, "rows", axis=0, tiled=True),
        lax.all_gather(narrow_key, "rows", axis=0, tiled=True),
        lax.all_gather(narrow_value, "rows", axis=0, tiled=True),
    )
    final_query, final_key, final_value = (final_query.T, final_key.T, final_value.T)
    serve_norm = lax.all_gather(
        (norm_train + norm_step).astype(jnp.bfloat16), ("rows", "tp"), axis=0, tiled=True
    )
    return (final_query, final_key, final_value, serve_norm)


def solution(mesh):
    in_specs = (
        P(("unit", "rows"), "tp"),
        P(("unit", "rows"), None),
        P("unit", "tp"),
        P(("unit", "rows"), "tp"),
        P(("unit", "rows"), None),
        P("unit", "tp"),
        P(("unit", "rows"), "tp"),
        P(("unit", "rows"), None),
        P("unit", "tp"),
        P(("unit", "rows", "tp")),
        P(("unit", "rows", "tp")),
    )
    out_specs = (
        P(("unit", "tp"), None),
        P(("unit", "tp"), None),
        P(("unit", "tp"), None),
        P("unit"),
    )
    return jax.shard_map(shards, mesh=mesh, in_specs=in_specs, out_specs=out_specs, check_vma=False)
```

profile of v0, /device:TPU:0, one launch (start us, length us, event | category | flops | bytes accessed | tf_op | source)
XLA Modules:
  0.0 108.7 jit_solution(17795586656834404858)
XLA Ops:
  7.2 0.0 copy-start
  7.2 0.0 copy-start.1
  7.2 0.0 copy-start.2
  7.2 0.0 copy-start.3
  7.2 0.0 all-gather.3.cloned.1.call-start
  7.3 0.8 copy-done
  8.0 2.2 %fusion.1 = bf16[512,512]{1,0:T(8,128)(2,1)} fusion(bf16[512,64]{0,1:T(8,128)(2,1)S(1)} %copy-done, bf16[64,512]{1,0:T(8,128)(2,1)} %param.13, bf16[512,512]{1,0:T(8,128)(2,1)} %param.11), kind=kOutput, calls=%fused_computation.2 | convolution fusion | flops 34603008 | bytes 1179648 | tf_op jit(solution)/shard_map/dot_general | solution.py:22
  10.2 0.0 all-gather.3.cloned.1.call-update
  10.2 0.0 copy-start.4
  10.2 0.0 copy-start.5
  10.3 1.2 %fusion.4 = bf16[512,128]{1,0:T(8,128)(2,1)S(1)} fusion(bf16[512,64]{0,1:T(8,128)(2,1)} %param.15, bf16[64,128]{1,0:T(8,128)(2,1)} %param.16, bf16[512,128]{1,0:T(8,128)(2,1)} %param.14), kind=kOutput, calls=%fused_computation.7 | convolution fusion | flops 8650752 | bytes 344064 | tf_op jit(solution)/shard_map/dot_general | solution.py:25
  11.4 22.0 %all_gather.13 = bf16[2048,128]{1,0:T(8,128)(2,1)S(1)} all-gather(bf16[512,128]{1,0:T(8,128)(2,1)S(1)} %fusion.4), channel_id=1, replica_groups=mesh['rows'=4,'tp'=4,'unit'=2] {'rows'}, dimensions={0}, use_global_device_ids=true | all-gather | bytes 655360 | tf_op jit(solution)/shard_map/all_gather | solution.py:38
  33.4 1.0 copy.22
  34.4 0.0 copy-done.1
  34.5 0.0 copy-done.2
  34.5 0.0 copy-done.3
  34.5 0.2 fusion.5
  34.7 21.7 %all_gather.14 = bf16[2048,128]{1,0:T(8,128)(2,1)S(1)} all-gather(bf16[512,128]{1,0:T(8,128)(2,1)S(1)} %fusion.5), channel_id=1, replica_groups=mesh['rows'=4,'tp'=4,'unit'=2] {'rows'}, dimensions={0}, use_global_device_ids=true | all-gather | bytes 655360 | tf_op jit(solution)/shard_map/all_gather | solution.py:39
  56.4 1.0 copy.23
  57.4 0.0 copy-done.4
  57.4 0.0 copy-done.5
  57.4 39.9 %all-gather = bf16[16,1,128]{2,1,0:T(2,128)(2,1)S(1)} all-gather(bf16[1,1,128]{2,1,0:T(2,128)(2,1)S(1)} %convert_bitcast_fusion), channel_id=1, replica_groups=mesh['rows'=4,'tp'=4,'unit'=2] {'rows','tp'}, dimensions={0}, use_global_device_ids=true | all-gather | bytes 4352 | tf_op jit(solution)/shard_map/all_gather | solution.py:42
  97.3 0.6 reduce
  98.0 3.9 %copy.21 = bf16[512,2048]{1,0:T(8,128)(2,1)} copy(bf16[512,2048]{0,1:T(8,128)(2,1)} %bitcast.14) | data formatting | bytes 4194304
  (2 shorter events, 0.0 us)
Async XLA Ops:
  7.2 0.8 copy-start
  7.2 27.3 %copy-start.1 = (bf16[512,128]{1,0:T(8,128)(2,1)S(1)}, bf16[512,128]{1,0:T(8,128)(2,1)}, u32[]{:S(2)}) copy-start(bf16[512,128]{1,0:T(8,128)(2,1)} %param.17) | copy-start | bytes 393220
  7.2 27.3 %copy-start.2 = (bf16[512,64]{0,1:T(8,128)(2,1)S(1)}, bf16[512,64]{0,1:T(8,128)(2,1)}, u32[]{:S(2)}) copy-start(bf16[512,64]{0,1:T(8,128)(2,1)} %param.18) | copy-start | bytes 196612
  7.2 27.3 %copy-start.3 = (bf16[64,128]{1,0:T(8,128)(2,1)S(1)}, bf16[64,128]{1,0:T(8,128)(2,1)}, u32[]{:S(2)}) copy-start(bf16[64,128]{1,0:T(8,128)(2,1)} %param.19) | copy-start | bytes 49156
  7.2 90.7 %all-gather.3.cloned.1.call-start = ((), (), s32[]{:S(2)}) async-start(), calls=%async_computation | async-start | bytes 2621440 | tf_op jit(solution)/shard_map/all_gather | solution.py:37
  10.2 47.2 %copy-start.4 = (f32[128]{0:T(128)S(1)}, f32[128]{0:T(128)}, u32[]{:S(2)}) copy-start(f32[128]{0:T(128)} %param.20) | copy-start | bytes 1540
  10.2 47.2 %copy-start.5 = (f32[128]{0:T(128)S(1)}, f32[128]{0:T(128)}, u32[]{:S(2)}) copy-start(f32[128]{0:T(128)} %param.21) | copy-start | bytes 1540
Sparse Core Ops, SparseCore 0:
  10.3 60.1 all-gather.2
where the time goes:
time: 109 us
  blocking collectives  83.6 us (77%)
  between operations  14.1 us (13%)
  local copies, waits for them, and re-layouts  6.71 us (6%)
  matrix products  3.58 us (3%)
    all_gather x1, blocking collectives, shards(): lax.all_gather((norm_train + norm_step).astype(jnp.bfloat16), ('rows', 't...  39.9 us
    all_gather x1, blocking collectives, shards(): lax.all_gather(narrow_key, 'rows', axis=0, tiled=True)  22 us
    all_gather x1, blocking collectives, shards(): lax.all_gather(narrow_value, 'rows', axis=0, tiled=True)  21.7 us
    unnamed x15, local copies, waits for them, and re-layouts  6.71 us
    dot_general x1, matrix products, shards(): jnp.dot(low_query, high_query, preferred_element_type=jnp.float32)  2.19 us
  transfers between devices with their start and end apart: 1, of which 0 were waited for; matrix products, arithmetic and copies ran while one was open for 4% of the time, Pallas kernels for 0%

commit v1 on v0

v1 whole, which is shorter than its diff:
```python
import functools

import jax
import jax.numpy as jnp
from jax import lax
from jax.experimental import pallas as pl
from jax.experimental.pallas import tpu as pltpu
from jax.sharding import PartitionSpec as P

mix_rate = 0.5
MESH = pl.DeviceIdType.MESH
LANES = 128


def kernel(
    n,
    peers,
    rows,
    *refs,
):
    (tq, lq, hq, tk, lk, hk, tv, lv, hv, norm_train, norm_step) = refs[:11]
    (oq, ok, ov, out_norm) = refs[11:15]
    held = refs[15:26]
    (gains, in_sem, send_sem, recv_sem, peer_send, peer_recv) = refs[26:]
    outs = (oq, ok, ov)
    me, part = lax.axis_index("rows"), lax.axis_index("tp")
    right, left = lax.rem(me + 1, n), lax.rem(me + n - 1, n)
    has_right, has_left = me < n - 1, me > 0

    barrier = pltpu.get_barrier_semaphore()

    def greet(axis, index):
        pl.semaphore_signal(barrier, inc=1, device_id={axis: index}, device_id_type=MESH)

    loads = [
        pltpu.make_async_copy(source, target, in_sem.at[i])
        for i, (source, target) in enumerate(zip(refs[:11], held))
    ]

    @pl.when(has_right)
    def _():
        greet("rows", right)

    @pl.when(has_left)
    def _():
        greet("rows", left)

    for step in range(1, peers):
        greet("tp", lax.rem(part + step, peers))
    for i in (1, 2, 0, 4, 5, 3, 7, 8, 6, 9, 10):
        loads[i].start()

    pieces = []
    for which, out in enumerate(outs):
        height = out.shape[-2]
        width = LANES if height % LANES == 0 else height
        pieces += [(which, start, width) for start in range(0, height, width)]
    norm_piece = len(pieces)

    def view(c, k):
        if c == norm_piece:
            return gains.at[k]
        which, start, width = pieces[c]
        out = outs[which]
        if len(out.shape) == 3:
            return out.at[k, pl.ds(start, width), :]
        return out.at[pl.ds(start, width), pl.ds(pl.multiple_of(k * rows, rows), rows)]

    def hop(c, k, way):
        return pltpu.make_async_remote_copy(
            src_ref=view(c, k),
            dst_ref=view(c, k),
            send_sem=send_sem.at[way, k, c],
            recv_sem=recv_sem.at[k, c],
            device_id={"rows": left if way else right},
            device_id_type=MESH,
        )

    def both_ways(c):
        @pl.when(has_right)
        def _():
            hop(c, me, 0).start()

        @pl.when(has_left)
        def _():
            hop(c, me, 1).start()

    ready = set()

    def merge(c):
        which, start, width = pieces[c]
        train, low, high = held[3 * which : 3 * which + 3]
        if which not in ready:
            ready.add(which)
            for i in (1, 2, 0):
                loads[3 * which + i].wait()
        span = pl.ds(start, width)
        product = lax.dot_general(
            high[:, span], low[...], (((0,), (0,)), ((), ())), preferred_element_type=jnp.float32
        )
        result = train[:, span].T.astype(jnp.float32) + mix_rate * product
        view(c, me)[...] = result.astype(jnp.bfloat16)

    merge(0)
    merge(1)
    pl.semaphore_wait(
        barrier, peers - 1 + has_right.astype(jnp.int32) + has_left.astype(jnp.int32)
    )
    both_ways(0)
    for c in range(2, norm_piece):
        merge(c)
        both_ways(c - 1)
    loads[9].wait()
    loads[10].wait()
    gains[me, part] = held[9][...] + held[10][...]
    both_ways(norm_piece - 1)

    def to_peer(step):
        return pltpu.make_async_remote_copy(
            src_ref=gains.at[me, part],
            dst_ref=gains.at[me, part],
            send_sem=peer_send.at[step],
            recv_sem=peer_recv.at[step],
            device_id={"tp": lax.rem(part + step, peers)},
            device_id_type=MESH,
        )

    for step in range(1, peers):
        to_peer(step).start()
    for step in range(1, peers):
        to_peer(step).wait()
    both_ways(norm_piece)

    def pass_on(step, carry):
        for c in range(norm_piece + 1):

            @pl.when(me - step >= 0)
            def _():
                hop(c, me - step, 0).wait_recv()

                @pl.when(has_right)
                def _():
                    hop(c, me - step, 0).start()

            @pl.when(me + step < n)
            def _():
                hop(c, me + step, 1).wait_recv()

                @pl.when(has_left)
                def _():
                    hop(c, me + step, 1).start()

        return carry

    lax.fori_loop(1, n, pass_on, 0)
    for k in range(n):
        for t in range(peers):
            out_norm[k * peers + t : k * peers + t + 1, :] = gains[k, t]

    def sent(step, carry):
        for c in range(norm_piece + 1):

            @pl.when((me - step >= 0) & has_right)
            def _():
                hop(c, me - step, 0).wait_send()

            @pl.when((me + step < n) & has_left)
            def _():
                hop(c, me + step, 1).wait_send()

        return carry

    lax.fori_loop(0, n, sent, 0)


def solution(mesh):
    n, peers = mesh.shape["rows"], mesh.shape["tp"]

    def shards(tq, lq, hq, tk, lk, hk, tv, lv, hv, norm_train, norm_step):
        rows = tq.shape[0]
        whole_tiles = rows % LANES == 0
        trains = (tq, tk, tv)
        operands = (
            tq, lq.T, hq, tk, lk.T, hk, tv, lv.T, hv,
            norm_train.reshape(1, -1), norm_step.reshape(1, -1),
        )
        heights = [train.shape[1] for train in trains]
        shapes = [
            (height, n * rows) if whole_tiles else (n, height, rows) for height in heights
        ]
        pieces = 1 + sum(h // LANES if h % LANES == 0 else 1 for h in heights)
        width = norm_train.shape[0]
        outs = pl.pallas_call(
            functools.partial(kernel, n, peers, rows),
            out_shape=[jax.ShapeDtypeStruct(shape, jnp.bfloat16) for shape in shapes]
            + [jax.ShapeDtypeStruct((n * peers, width), jnp.float32)],
            in_specs=[pl.BlockSpec(memory_space=pl.ANY)] * len(operands),
            out_specs=[pl.BlockSpec(memory_space=pltpu.VMEM)] * 4,
            scratch_shapes=[pltpu.VMEM(x.shape, x.dtype) for x in operands]
            + [
                pltpu.VMEM((n, peers, 1, width), jnp.float32),
                pltpu.SemaphoreType.DMA((len(operands),)),
                pltpu.SemaphoreType.DMA((2, n, pieces)),
                pltpu.SemaphoreType.DMA((n, pieces)),
                pltpu.SemaphoreType.DMA((peers,)),
                pltpu.SemaphoreType.DMA((peers,)),
            ],
            compiler_params=pltpu.CompilerParams(collective_id=0, has_side_effects=True),
        )(*operands)
        finals = [
            out if whole_tiles else out.transpose(1, 0, 2).reshape(height, n * rows)
            for out, height in zip(outs, heights)
        ]
        return (*finals, outs[3].astype(jnp.bfloat16).reshape(-1))

    in_specs = (
        P(("unit", "rows"), "tp"),
        P(("unit", "rows"), None),
        P("unit", "tp"),
    ) * 3 + (P(("unit", "rows", "tp")),) * 2
    out_specs = (P(("unit", "tp"), None),) * 3 + (P("unit"),)
    return jax.shard_map(shards, mesh=mesh, in_specs=in_specs, out_specs=out_specs, check_vma=False)
```

time: 109 us -> 66.3 us (0.61)
  blocking collectives: 83.6 us -> 0 us
  Pallas kernels: 0 us -> 59.3 us
  between operations: 14.1 us -> 0.65 us
  matrix products: 3.58 us -> 0 us
  local copies, waits for them, and re-layouts: 6.71 us -> 4.84 us
    all_gather x3 -> x0, blocking collectives: 83.6 us -> none  [the longest x1 39.9 us: shards(): lax.all_gather((norm_train + norm_step).astype(jnp.bfloat16), ('rows', 't...]
    pallas_call x0 -> x1, Pallas kernels: none -> 59.3 us  [shards(): pl.pallas_call(functools.partial(kernel, n, peers, rows), out_shape=[jax....]
    dot_general x3 -> x0, matrix products: 3.58 us -> none  [the longest x1 2.19 us: shards(): jnp.dot(low_query, high_query, preferred_element_type=jnp.float32)]
    unnamed x15 -> x7, local copies, waits for them, and re-layouts: 6.71 us -> 4.84 us
    reshape x0 -> x1, other arithmetic: none -> 1.29 us  [shards(): return (*finals, outs[3].astype(jnp.bfloat16).reshape(-1))]
  transfers between devices with their start and end apart: 1 -> 0, of which waited for: 0 -> 0; matrix products, arithmetic and copies ran while one was open for 4% -> 0% of each run, Pallas kernels for 0% -> 0%
where the time goes in v1:
time: 66.3 us; the launch traced here: 66.1 us
  Pallas kernels  59.3 us (89%)
  local copies, waits for them, and re-layouts  4.84 us (7%)
  other arithmetic  1.29 us (2%)
    pallas_call x1, Pallas kernels, shards(): pl.pallas_call(functools.partial(kernel, n, peers, rows), out_shape=[jax....  59.3 us
    unnamed x7, local copies, waits for them, and re-layouts  4.84 us

profile of v1, /device:TPU:0, one launch (start us, length us, event | category | flops | bytes accessed | tf_op | source)
XLA Modules:
  0.0 66.1 jit_solution(14983673703339664540)
XLA Ops:
  0.6 59.3 %shard_map.138 = (bf16[512,2048]{1,0:T(8,128)(2,1)}, bf16[128,2048]{1,0:T(8,128)(2,1)}, bf16[128,2048]{1,0:T(8,128)(2,1)}, f32[16,128]{1,0:T(8,128)}) custom-call(bf16[512,512]{1,0:T(8,128)(2,1)} %refs_0_.1, bf16[64,512]{1,0:T(8,128)(2,1)} %bitcast.7, bf16[64,512]{1,0:T(8,128)(2,1)} %refs_2_.1, bf16[512,128]{1,0:T(8,128)(2,1)} %refs_3_.1, ...), custom_call_target="tpu_custom_call" | custom-call | tf_op jit(solution)/shard_map/pallas_call | solution.py:193
  59.9 1.3 %convert_bitcast_fusion = bf16[2048]{0:T(1024)(128)(2,1)} fusion(f32[16,128]{1,0:T(8,128)} %get-tuple-element.11), kind=kLoop, calls=%fused_computation | loop fusion | flops 2048 | bytes 12288 | tf_op jit(solution)/shard_map/reshape | solution.py:214
  61.2 0.0 copy-start.1
  61.2 0.0 copy-start
  61.2 3.2 %copy.18 = bf16[512,2048]{1,0:T(8,128)(2,1)} copy(bf16[512,2048]{1,0:T(8,128)(2,1)} %get-tuple-element.16) | data formatting | bytes 4194304
  64.5 0.0 copy-done.1
  64.5 0.8 %copy.19 = bf16[128,2048]{1,0:T(8,128)(2,1)} copy(bf16[128,2048]{1,0:T(8,128)(2,1)S(1)} %copy-done.1) | data formatting | bytes 1048576
  65.3 0.0 copy-done
  65.3 0.8 %copy.20 = bf16[128,2048]{1,0:T(8,128)(2,1)} copy(bf16[128,2048]{1,0:T(8,128)(2,1)S(1)} %copy-done) | data formatting | bytes 1048576
Async XLA Ops:
  61.2 3.3 %copy-start.1 = (bf16[128,2048]{1,0:T(8,128)(2,1)S(1)}, bf16[128,2048]{1,0:T(8,128)(2,1)}, u32[]{:S(2)}) copy-start(bf16[128,2048]{1,0:T(8,128)(2,1)} %get-tuple-element.17) | copy-start | bytes 1572868
  61.2 4.0 %copy-start = (bf16[128,2048]{1,0:T(8,128)(2,1)S(1)}, bf16[128,2048]{1,0:T(8,128)(2,1)}, u32[]{:S(2)}) copy-start(bf16[128,2048]{1,0:T(8,128)(2,1)} %get-tuple-element.18) | copy-start | bytes 1572868

commit v2 on v1

--- a/solution.py
+++ b/solution.py
@@ -192,7 +192,10 @@
         width = norm_train.shape[0]
         outs = pl.pallas_call(
             functools.partial(kernel, n, peers, rows),
-            out_shape=[jax.ShapeDtypeStruct(shape, jnp.bfloat16) for shape in shapes]
+            out_shape=[
+                (pltpu.VMEM if whole_tiles else jax.ShapeDtypeStruct)(shape, jnp.bfloat16)
+                for shape in shapes
+            ]
             + [jax.ShapeDtypeStruct((n * peers, width), jnp.float32)],
             in_specs=[pl.BlockSpec(memory_space=pl.ANY)] * len(operands),
             out_specs=[pl.BlockSpec(memory_space=pltpu.VMEM)] * 4,

time: 66.3 us -> 62.5 us (0.943)
  local copies, waits for them, and re-layouts: 4.84 us -> 2.91 us
  Pallas kernels: 59.3 us -> 58.2 us
  other arithmetic: 1.29 us -> 0.59 us
    unnamed x7 -> x5, local copies, waits for them, and re-layouts: 4.84 us -> 2.91 us
    pallas_call x1, Pallas kernels: 59.3 us -> 58.2 us  [shards(): pl.pallas_call(functools.partial(kernel, n, peers, rows), out_shape=[(plt...]
    reshape x1, other arithmetic: 1.29 us -> 0.59 us  [shards(): return (*finals, outs[3].astype(jnp.bfloat16).reshape(-1))]
where the time goes in v2:
time: 62.5 us; the launch traced here: 62.4 us
  Pallas kernels  58.2 us (93%)
  local copies, waits for them, and re-layouts  2.91 us (5%)
  between operations  0.65 us (1%)
    pallas_call x1, Pallas kernels, shards(): pl.pallas_call(functools.partial(kernel, n, peers, rows), out_shape=[(plt...  58.2 us
    unnamed x5, local copies, waits for them, and re-layouts  2.91 us

profile of v2, /device:TPU:0, one launch (start us, length us, event | category | flops | bytes accessed | tf_op | source)
XLA Modules:
  0.0 62.4 jit_solution(13559038578025894552)
XLA Ops:
  0.6 58.2 %shard_map.138 = (bf16[512,2048]{1,0:T(8,128)(2,1)S(1)}, bf16[128,2048]{1,0:T(8,128)(2,1)S(1)}, bf16[128,2048]{1,0:T(8,128)(2,1)S(1)}, f32[16,128]{1,0:T(8,128)}) custom-call(bf16[512,512]{1,0:T(8,128)(2,1)} %refs_0_.1, bf16[64,512]{1,0:T(8,128)(2,1)} %bitcast.7, bf16[64,512]{1,0:T(8,128)(2,1)} %refs_2_.1, bf16[512,128]{1,0:T(8,128)(2,1)} %refs_3_.1, ...), custom_call_target="tpu_custom_call" | custom-call | tf_op jit(solution)/shard_map/pallas_call | solution.py:193
  58.9 0.0 copy-start
  58.9 1.3 %copy.18 = bf16[512,2048]{1,0:T(8,128)(2,1)} copy(bf16[512,2048]{1,0:T(8,128)(2,1)S(1)} %get-tuple-element.12) | data formatting | bytes 4194304
  60.2 0.0 copy-done
  60.2 0.6 convert_bitcast_fusion
  60.8 0.8 %copy.19 = bf16[128,2048]{1,0:T(8,128)(2,1)} copy(bf16[128,2048]{1,0:T(8,128)(2,1)S(1)} %get-tuple-element.13) | data formatting | bytes 1048576
  61.6 0.8 %copy.20 = bf16[128,2048]{1,0:T(8,128)(2,1)} copy(bf16[128,2048]{1,0:T(8,128)(2,1)S(1)} %get-tuple-element.14) | data formatting | bytes 1048576
Async XLA Ops:
  58.9 1.3 %copy-start = (f32[16,128]{1,0:T(8,128)S(1)}, f32[16,128]{1,0:T(8,128)}, u32[]{:S(2)}) copy-start(f32[16,128]{1,0:T(8,128)} %get-tuple-element.11) | copy-start | bytes 24580

commit v3 on v1

--- a/solution.py
+++ b/solution.py
@@ -21,7 +21,7 @@
     (tq, lq, hq, tk, lk, hk, tv, lv, hv, norm_train, norm_step) = refs[:11]
     (oq, ok, ov, out_norm) = refs[11:15]
     held = refs[15:26]
-    (gains, in_sem, send_sem, recv_sem, peer_send, peer_recv) = refs[26:]
+    (gains, sums, in_sem, send_sem, recv_sem, peer_send, peer_recv) = refs[26:]
     outs = (oq, ok, ov)
     me, part = lax.axis_index("rows"), lax.axis_index("tp")
     right, left = lax.rem(me + 1, n), lax.rem(me + n - 1, n)
@@ -155,7 +155,8 @@
     lax.fori_loop(1, n, pass_on, 0)
     for k in range(n):
         for t in range(peers):
-            out_norm[k * peers + t : k * peers + t + 1, :] = gains[k, t]
+            sums[k * peers + t : k * peers + t + 1, :] = gains[k, t]
+    out_norm[...] = sums[...].astype(jnp.bfloat16)
 
     def sent(step, carry):
         for c in range(norm_piece + 1):
@@ -171,6 +172,19 @@
         return carry
 
     lax.fori_loop(0, n, sent, 0)
+
+
+def settle(*refs):
+    *arrays, sem = refs
+    half = len(arrays) // 2
+    copies = [
+        pltpu.make_async_copy(source, target, sem.at[i])
+        for i, (source, target) in enumerate(zip(arrays[:half], arrays[half:]))
+    ]
+    for copy in copies:
+        copy.start()
+    for copy in copies:
+        copy.wait()
 
 
 def solution(mesh):
@@ -190,15 +204,18 @@
         ]
         pieces = 1 + sum(h // LANES if h % LANES == 0 else 1 for h in heights)
         width = norm_train.shape[0]
+        place = pltpu.VMEM if whole_tiles else jax.ShapeDtypeStruct
         outs = pl.pallas_call(
             functools.partial(kernel, n, peers, rows),
-            out_shape=[jax.ShapeDtypeStruct(shape, jnp.bfloat16) for shape in shapes]
-            + [jax.ShapeDtypeStruct((n * peers, width), jnp.float32)],
+            out_shape=[
+                place(shape, jnp.bfloat16) for shape in (*shapes, (n * peers, width))
+            ],
             in_specs=[pl.BlockSpec(memory_space=pl.ANY)] * len(operands),
             out_specs=[pl.BlockSpec(memory_space=pltpu.VMEM)] * 4,
             scratch_shapes=[pltpu.VMEM(x.shape, x.dtype) for x in operands]
             + [
                 pltpu.VMEM((n, peers, 1, width), jnp.float32),
+                pltpu.VMEM((n * peers, width), jnp.float32),
                 pltpu.SemaphoreType.DMA((len(operands),)),
                 pltpu.SemaphoreType.DMA((2, n, pieces)),
                 pltpu.SemaphoreType.DMA((n, pieces)),
@@ -207,11 +224,21 @@
             ],
             compiler_params=pltpu.CompilerParams(collective_id=0, has_side_effects=True),
         )(*operands)
+        if whole_tiles:
+            *finals, norm = pl.pallas_call(
+                settle,
+                out_shape=[jax.ShapeDtypeStruct(out.shape, out.dtype) for out in outs],
+                in_specs=[pl.BlockSpec(memory_space=pltpu.VMEM)] * len(outs),
+                out_specs=[pl.BlockSpec(memory_space=pl.ANY)] * len(outs),
+                scratch_shapes=[pltpu.SemaphoreType.DMA((len(outs),))],
+                compiler_params=pltpu.CompilerParams(vmem_limit_bytes=8 * 1024 * 1024),
+            )(*outs)
+            return (*finals, norm.reshape(-1))
         finals = [
-            out if whole_tiles else out.transpose(1, 0, 2).reshape(height, n * rows)
+            out.transpose(1, 0, 2).reshape(height, n * rows)
             for out, height in zip(outs, heights)
         ]
-        return (*finals, outs[3].astype(jnp.bfloat16).reshape(-1))
+        return (*finals, outs[3].reshape(-1))
 
     in_specs = (
         P(("unit", "rows"), "tp"),

time: 66.3 us -> 60.1 us (0.906)
  local copies, waits for them, and re-layouts: 4.84 us -> 0 us
  other arithmetic: 1.29 us -> 0 us
    unnamed x7 -> x0, local copies, waits for them, and re-layouts: 4.84 us -> none
    reshape x1 -> x0, other arithmetic: 1.29 us -> none  [shards(): return (*finals, outs[3].astype(jnp.bfloat16).reshape(-1))]
    pallas_call x1 -> x2, Pallas kernels: 59.3 us -> 59.3 us  [the longest x1 57.6 us: shards(): pl.pallas_call(functools.partial(kernel, n, peers, rows), out_shape=[plac...]
where the time goes in v3:
time: 60.1 us; the launch traced here: 60 us
  Pallas kernels  59.3 us (99%)
  between operations  0.64 us (1%)
    pallas_call x1, Pallas kernels, shards(): pl.pallas_call(functools.partial(kernel, n, peers, rows), out_shape=[plac...  57.6 us
    pallas_call x1, Pallas kernels, shards(): pl.pallas_call(settle, out_shape=[jax.ShapeDtypeStruct(out.shape, out.dty...  1.7 us

profile of v3, /device:TPU:0, one launch (start us, length us, event | category | flops | bytes accessed | tf_op | source)
XLA Modules:
  0.0 60.0 jit_solution(858961011820611757)
XLA Ops:
  0.6 57.6 %shard_map.138 = (bf16[512,2048]{1,0:T(8,128)(2,1)S(1)}, bf16[128,2048]{1,0:T(8,128)(2,1)S(1)}, bf16[128,2048]{1,0:T(8,128)(2,1)S(1)}, bf16[16,128]{1,0:T(8,128)(2,1)S(1)}) custom-call(bf16[512,512]{1,0:T(8,128)(2,1)} %refs_0_.1, bf16[64,512]{1,0:T(8,128)(2,1)} %bitcast.6, bf16[64,512]{1,0:T(8,128)(2,1)} %refs_2_.1, bf16[512,128]{1,0:T(8,128)(2,1)} %refs_3_.1, ...), custom_call_target="tpu_custom_call" | custom-call | tf_op jit(solution)/shard_map/pallas_call | solution.py:208
  58.3 1.7 %shard_map.139 = (bf16[512,2048]{1,0:T(8,128)(2,1)}, bf16[128,2048]{1,0:T(8,128)(2,1)}, bf16[128,2048]{1,0:T(8,128)(2,1)}, bf16[16,128]{1,0:T(8,128)(2,1)}) custom-call(bf16[512,2048]{1,0:T(8,128)(2,1)S(1)} %get-tuple-element.12.refs_0_, bf16[128,2048]{1,0:T(8,128)(2,1)S(1)} %get-tuple-element.13.refs_1_, bf16[128,2048]{1,0:T(8,128)(2,1)S(1)} %get-tuple-element.14.refs_2_, ...), custom_call_target="tpu_custom_call" | custom-call | tf_op jit(solution)/shard_map/pallas_call | solution.py:228
